TPU v7x, 128 devices: a whole 4x4x4 slice. The times are simulated.
128 devices in a mesh: dp: 8 (over y, core), tp: 16 (over z, x).
Axes of the slice: x: 4, y: 4, z: 4, core: 2. Of those that a mesh axis runs over, the one named last changes fastest.
Arguments:
- tokens: bfloat16 [10240, 6144], P(('dp', 'tp')), parts along dimension 0, may hold values from -6 to 6
- ln_gain: float32 [6144], replicated, may hold values from 0.25 to 1.75
- ln_bias: float32 [6144], replicated, may hold values from -1.75 to 1.75
- w_qkv: bfloat16 [6144, 3, 6144], P(None, None, 'tp'), may hold values from -0.45927933 to 0.45927933
- b_qkv: float32 [3, 6144], P(None, 'tp'), may hold values from -3 to 3
- w_out: bfloat16 [6144, 6144], P('tp'), may hold values from -0.078125 to 0.078125
- b_out: float32 [6144], replicated, may hold values from -1.25 to 1.25
- kv_cache: bfloat16 [2, 96, 128, 6144], P(None, 'dp', None, 'tp'), parts along dimension 1, may hold values from -6 to 6
- page_table: int32 [8, 10], P('dp'), parts along dimension 0, may hold values from 0 to 11, as said below
- lengths: int32 [8], P('dp'), parts along dimension 0, may hold values from 641 to 1280
Outputs:
- attn_out: bfloat16 [10240, 6144], P(('dp', 'tp')), parts along dimension 0
- kv_cache_out: bfloat16 [2, 96, 128, 6144], P(None, 'dp', None, 'tp'), parts along dimension 1
There are 8 independent parts, one for each index of `dp`. A program takes and returns all parts, laid end to end along the dimension named above; an argument that names none is the same for every part. Nothing has to cross between parts.
Inputs may be any that keep to these rules, and one draw needn't show every extreme that they name: `page_table`: no slot is named twice within a part.
All inputs are finite; a program needn't handle non-finite values.
Results may differ from a plain program's by a relative error of at most 0.015.
The roundings to bfloat16 on the way count: a program that leaves them out, or rounds other values in their place, can miss the bound.
Values may be sent and summed in bfloat16 or wider, within the bound.
A program may use at most 128 MiB of HBM per device.

v0:
```python
import math
import jax
import jax.numpy as jnp
from jax import lax
from jax.sharding import PartitionSpec as P

HD = 128
SEQS = 1
norm_eps = 1e-05


def layer_norm(token_rows, gain_row, shift_row):
    floats = token_rows.astype(jnp.float32)
    center = jnp.mean(floats, axis=-1, keepdims=True)
    spread = jnp.mean(jnp.square(floats - center), axis=-1, keepdims=True)
    return ((floats - center) * lax.rsqrt(spread + norm_eps) * gain_row + shift_row).astype(
        jnp.bfloat16
    )


def attend(queries, keys, values, lengths):
    seq_count, seq_len, head_count, head_dim = queries.shape
    block_len = math.gcd(seq_len, 512)
    score_scale = 1.0 / math.sqrt(head_dim)
    key_pos = jnp.arange(seq_len, dtype=jnp.int32)

    def one_sequence(inputs):
        seq_query, seq_key, seq_value, length = inputs
        blocks = seq_query.reshape(seq_len // block_len, block_len, head_count, head_dim)

        def one_block(block_pair):
            block_query, block_index = block_pair
            scores = (
                jnp.einsum("qhe,khe->hqk", block_query, seq_key, preferred_element_type=jnp.float32)
                * score_scale
            )
            query_pos = block_index * block_len + jnp.arange(block_len, dtype=jnp.int32)
            allowed = (key_pos[None, :] <= query_pos[:, None]) & (key_pos[None, :] < length)
            scores = jnp.where(allowed[None], scores, -1e30)
            row_max = jnp.max(scores, axis=-1, keepdims=True)
            raised = jnp.exp(scores - row_max)
            weights = (raised / jnp.sum(raised, axis=-1, keepdims=True)).astype(jnp.bfloat16)
            return jnp.einsum(
                "hqk,khe->qhe", weights, seq_value, preferred_element_type=jnp.float32
            ).astype(jnp.bfloat16)

        results = lax.map(one_block, (blocks, jnp.arange(seq_len // block_len, dtype=jnp.int32)))
        return results.reshape(seq_len, head_count, head_dim)

    return lax.map(one_sequence, (queries, keys, values, lengths))


def write_cache(kv_cache, key_value, page_table, lengths):
    seq_count, page_count = page_table.shape
    page_len = kv_cache.shape[2]
    feat_here = kv_cache.shape[3]
    fresh_pages = jnp.moveaxis(key_value, 1, 0).reshape(
        2, seq_count * page_count, page_len, feat_here
    )
    slot_ids = page_table.reshape(-1)
    positions = (
        jnp.arange(page_count, dtype=jnp.int32)[:, None] * page_len
        + jnp.arange(page_len, dtype=jnp.int32)[None, :]
    )
    written = (positions[None] < lengths[:, None, None]).reshape(seq_count * page_count, page_len)
    current = kv_cache[:, slot_ids]
    new_pages = jnp.where(written[None, :, :, None], fresh_pages, current)
    return kv_cache.at[:, slot_ids].set(new_pages)


def body(tokens, ln_gain, ln_bias, w_qkv, b_qkv, w_out, b_out, kv_cache, page_table, lengths):
    model_width = tokens.shape[1]
    local_feat = w_qkv.shape[2]
    weights_flat = w_qkv.reshape(model_width, 3 * local_feat)
    bias_flat = b_qkv.reshape(-1)
    normed = layer_norm(tokens, ln_gain, ln_bias)
    block_rows = lax.all_gather(normed, "tp", axis=0, tiled=True)
    result = jnp.dot(block_rows, weights_flat, preferred_element_type=jnp.float32) + bias_flat
    projected = result.astype(jnp.bfloat16).reshape(block_rows.shape[0], 3, local_feat)
    all_rows = projected.shape[0]
    seq_len = all_rows // SEQS
    heads_here = local_feat // HD
    queries = projected[:, 0].reshape(SEQS, seq_len, heads_here, HD)
    keys = projected[:, 1].reshape(SEQS, seq_len, heads_here, HD)
    values = projected[:, 2].reshape(SEQS, seq_len, heads_here, HD)
    attended = attend(queries, keys, values, lengths).reshape(all_rows, local_feat)
    summed = lax.psum_scatter(
        jnp.dot(attended, w_out, preferred_element_type=jnp.float32).astype(jnp.bfloat16),
        "tp",
        scatter_dimension=0,
        tiled=True,
    ).astype(jnp.float32)
    attn_out = (summed + b_out).astype(jnp.bfloat16)
    kv_cache_out = write_cache(kv_cache, projected[:, 1:3], page_table, lengths)
    return (attn_out, kv_cache_out)


def solution(mesh):
    placed = (
        P(("dp", "tp"), None),
        P(),
        P(),
        P(None, None, "tp"),
        P(None, "tp"),
        P("tp", None),
        P(),
        P(None, "dp", None, "tp"),
        P("dp", None),
        P("dp"),
    )
    return jax.shard_map(
        body,
        mesh=mesh,
        in_specs=placed,
        out_specs=(P(("dp", "tp"), None), P(None, "dp", None, "tp")),
        check_vma=False,
    )
```

profile of v0, /device:TPU:0, one launch (start us, length us, event | category | flops | bytes accessed | tf_op | source)
XLA Modules:
  0.0 334.9 jit_solution(16525906927422556471)
XLA Ops:
  11.2 18.8 %copy.20 = bf16[6144,3,384]{0,2,1:T(8,128)(2,1)} copy(bf16[6144,3,384]{2,0,1:T(8,128)(2,1)} %param.15) | data formatting | bytes 28311552 | tf_op args[3]
  30.1 89.7 %all-gather.2.cloned.1.call-done = bf16[1280,6144]{1,0:T(8,128)(2,1)} async-done(((bf16[80,6144]{1,0:T(8,128)(2,1)}), bf16[1280,6144]{1,0:T(8,128)(2,1)}) %all-gather.2.cloned.1.call-update) | async-done | bytes 15728656 | tf_op jit(solution)/shard_map/all_gather | solution.py:77
  119.8 25.8 %fusion.37 = bf16[1280,1152]{0,1:T(8,128)(2,1)S(1)} fusion(bf16[1280,6144]{1,0:T(8,128)(2,1)} %all-gather.2.cloned.1.call-done, bf16[6144,1152]{0,1:T(8,128)(2,1)} %bitcast.67, f32[1152]{0:T(1024)S(1)} %add.87), kind=kOutput, calls=%fused_computation.32 | convolution fusion | flops 18122342400 | bytes 32838144 | tf_op jit(solution)/shard_map/dot_general | solution.py:78
  147.9 3.5 %reshape.187 = bf16[5,256,3,128]{1,0,3,2:T(8,128)(2,1)} reshape(bf16[1280,1,384]{0,2,1:T(8,128)(2,1)} %get-tuple-element.135) | data formatting | bytes 1966080 | tf_op jit(solution)/shard_map/while/body/eval_jaxpr/reshape | solution.py:29
  151.4 2.6 copy.22
  157.5 46.2 %while.19 = (s32[]{:T(128)}, bf16[5,256,3,128]{3,1,2,0:T(8,128)(2,1)}, s32[5]{0:T(128)S(1)}, s32[]{:T(128)}, bf16[5,256,3,128]{3,1,2,0:T(8,128)(2,1)}, /*index=5...) while((s32[]{:T(128)}, ...), condition=%wide.region_5.6_spmd.clone.clone, body=%wide.region_2.5_spmd.clone.clone.sunk | while | flops 764580608 | bytes 4534397 | solution.py:47
  159.5 2.9 fusion.72
  162.4 4.3 %fusion.73 = bf16[5,256,3,128]{3,1,2,0:T(8,128)(2,1)} fusion(bf16[5,256,3,128]{3,1,2,0:T(8,128)(2,1)} %get-tuple-element.189, s32[]{:T(128)} %get-tuple-element.188, bf16[1280,3,128]{2,0,1:T(8,128)(2,1)} %get-tuple-element.203, f32[3,256]{1,0:T(4,128)S(1)} %fusion.72, bf16[1280,3,128]{2,0,1:T(8,128)(2,1)} %get-tuple-element.202, ...), kind=kOutput, calls=%fused_computation.14.clone.1 | convolution fusion | flops 508332032 | bytes 2691072 | tf_op jit(solution)/shard_map/while/body/eval_jaxpr/while/body/eval_jaxpr/hqk,khe->qhe/dot_general | solution.py:43
  168.8 2.9 fusion.72
  171.6 4.3 %fusion.73 = bf16[5,256,3,128]{3,1,2,0:T(8,128)(2,1)} fusion(bf16[5,256,3,128]{3,1,2,0:T(8,128)(2,1)} %get-tuple-element.189, s32[]{:T(128)} %get-tuple-element.188, bf16[1280,3,128]{2,0,1:T(8,128)(2,1)} %get-tuple-element.203, f32[3,256]{1,0:T(4,128)S(1)} %fusion.72, bf16[1280,3,128]{2,0,1:T(8,128)(2,1)} %get-tuple-element.202, ...), kind=kOutput, calls=%fused_computation.14.clone.1 | convolution fusion | flops 508332032 | bytes 2691072 | tf_op jit(solution)/shard_map/while/body/eval_jaxpr/while/body/eval_jaxpr/hqk,khe->qhe/dot_general | solution.py:43
  178.0 2.9 fusion.72
  180.9 4.3 %fusion.73 = bf16[5,256,3,128]{3,1,2,0:T(8,128)(2,1)} fusion(bf16[5,256,3,128]{3,1,2,0:T(8,128)(2,1)} %get-tuple-element.189, s32[]{:T(128)} %get-tuple-element.188, bf16[1280,3,128]{2,0,1:T(8,128)(2,1)} %get-tuple-element.203, f32[3,256]{1,0:T(4,128)S(1)} %fusion.72, bf16[1280,3,128]{2,0,1:T(8,128)(2,1)} %get-tuple-element.202, ...), kind=kOutput, calls=%fused_computation.14.clone.1 | convolution fusion | flops 508332032 | bytes 2691072 | tf_op jit(solution)/shard_map/while/body/eval_jaxpr/while/body/eval_jaxpr/hqk,khe->qhe/dot_general | solution.py:43
  187.3 2.9 fusion.72
  190.1 4.3 %fusion.73 = bf16[5,256,3,128]{3,1,2,0:T(8,128)(2,1)} fusion(bf16[5,256,3,128]{3,1,2,0:T(8,128)(2,1)} %get-tuple-element.189, s32[]{:T(128)} %get-tuple-element.188, bf16[1280,3,128]{2,0,1:T(8,128)(2,1)} %get-tuple-element.203, f32[3,256]{1,0:T(4,128)S(1)} %fusion.72, bf16[1280,3,128]{2,0,1:T(8,128)(2,1)} %get-tuple-element.202, ...), kind=kOutput, calls=%fused_computation.14.clone.1 | convolution fusion | flops 508332032 | bytes 2691072 | tf_op jit(solution)/shard_map/while/body/eval_jaxpr/while/body/eval_jaxpr/hqk,khe->qhe/dot_general | solution.py:43
  196.5 2.9 fusion.72
  199.4 4.3 %fusion.73 = bf16[5,256,3,128]{3,1,2,0:T(8,128)(2,1)} fusion(bf16[5,256,3,128]{3,1,2,0:T(8,128)(2,1)} %get-tuple-element.189, s32[]{:T(128)} %get-tuple-element.188, bf16[1280,3,128]{2,0,1:T(8,128)(2,1)} %get-tuple-element.203, f32[3,256]{1,0:T(4,128)S(1)} %fusion.72, bf16[1280,3,128]{2,0,1:T(8,128)(2,1)} %get-tuple-element.202, ...), kind=kOutput, calls=%fused_computation.14.clone.1 | convolution fusion | flops 508332032 | bytes 2691072 | tf_op jit(solution)/shard_map/while/body/eval_jaxpr/while/body/eval_jaxpr/hqk,khe->qhe/dot_general | solution.py:43
  205.7 14.1 %convolution_convert_fusion = bf16[1280,6144]{1,0:T(8,128)(2,1)} fusion(bf16[384,6144]{1,0:T(8,128)(2,1)} %param.17, bf16[160,8,3,128]{3,2,1,0:T(4,128)(2,1)S(1)} %bitcast.73), kind=kOutput, calls=%fused_computation.30 | convolution fusion | flops 6047662080 | bytes 21430272 | tf_op jit(solution)/shard_map/dot_general | solution.py:88
  220.5 2.2 gather_fusion
  222.8 3.0 slice_bitcast_fusion
  225.8 4.0 %copy.26 = bf16[2,1280,384]{2,1,0:T(8,128)(2,1)} copy(bf16[2,1280,384]{1,2,0:T(8,128)(2,1)} %slice_bitcast_fusion) | data formatting | bytes 3932160 | tf_op jit(solution)/shard_map/transpose | solution.py:57
  229.8 3.7 %fusion.44 = bf16[10,2,128,384]{3,2,1,0:T(8,128)(2,1)} fusion(bf16[10,2,128,384]{3,2,1,0:T(8,128)(2,1)} %gather_fusion, bf16[2,10,128,384]{3,2,1,0:T(8,128)(2,1)} %bitcast.70, pred[10,128]{1,0:T(8,128)(4,1)S(1)} %add_compare_fusion), kind=kLoop, calls=%fused_computation.43 | loop fusion | flops 983040 | bytes 5899520 | tf_op jit(solution)/shard_map/jit(_where)/select_n | solution.py:67
  233.5 4.5 %scatter_fusion = bf16[2,12,128,384]{3,2,1,0:T(8,128)(2,1)S(1)} fusion(bf16[2,12,128,384]{3,2,1,0:T(8,128)(2,1)S(1)} %copy.47, s32[10]{0:T(128)S(1)} %fusion.47, bf16[10,2,128,384]{3,2,1,0:T(8,128)(2,1)} %fusion.44), kind=kCustom, calls=%fused_computation.1 | custom fusion | bytes 5898280 | tf_op jit(solution)/shard_map/scatter | solution.py:68
  238.0 87.7 %reduce-scatter.2.cloned.1.call-done = bf16[80,6144]{1,0:T(8,128)(2,1)} async-done(((bf16[1280,6144]{1,0:T(8,128)(2,1)}), bf16[80,6144]{1,0:T(8,128)(2,1)}) %reduce-scatter.2.cloned.1.call-update) | async-done | bytes 983056 | tf_op jit(solution)/shard_map/reduce_scatter | solution.py:87
  325.7 2.3 add_convert_fusion
  (57 shorter events, 19.5 us)
Async XLA Ops:
  7.2 1.9 copy-start.1
  7.2 2.6 copy-start.4
  7.2 2.6 copy-start.3
  7.2 112.6 %all-gather.2.cloned.1.call-start = ((), (), s32[]{:S(2)}) async-start(), calls=%async_computation.1 | async-start | bytes 16711680 | tf_op jit(solution)/shard_map/all_gather | solution.py:77
  11.2 314.5 %reduce-scatter.2.cloned.1.call-start = ((), (), s32[]{:S(2)}) async-start(), calls=%async_computation.2 | async-start | bytes 16711680 | tf_op jit(solution)/shard_map/reduce_scatter | solution.py:87
  11.2 18.8 %copy-start.6 = (f32[3,384]{1,0:T(4,128)S(1)}, f32[3,384]{1,0:T(4,128)}, u32[]{:S(2)}) copy-start(f32[3,384]{1,0:T(4,128)} %param.16) | copy-start | bytes 13828
  145.6 2.3 copy-start.2
  219.8 0.7 copy-start.7
  233.5 92.2 %copy-start.5 = (f32[6144]{0:T(1024)S(1)}, f32[6144]{0:T(1024)}, u32[]{:S(2)}) copy-start(f32[6144]{0:T(1024)} %param.18) | copy-start | bytes 73732
  238.0 90.0 %copy-start = (bf16[2,12,128,384]{3,2,1,0:T(8,128)(2,1)}, bf16[2,12,128,384]{3,2,1,0:T(8,128)(2,1)S(1)}, u32[]{:S(2)}) copy-start(bf16[2,12,128,384]{3,2,1,0:T(8,128)(2,1)S(1)} %scatter_fusion) | copy-start | bytes 7077892
Sparse Core Ops, SparseCore 0:
  11.3 108.4 all-gather.1
  219.9 105.7 reduce-scatter.1
where the time goes:
time: 336 us; the launch traced here: 335 us
  waiting for transfers between devices  177 us (53%)
  matrix products  75.7 us (23%)
  local copies, waits for them, and re-layouts  51 us (15%)
  between operations  14.8 us (4%)
  other arithmetic  12.9 us (4%)
    all_gather x1, waiting for transfers between devices, body(): block_rows = lax.all_gather(normed, 'tp', axis=0, tiled=True)  89.7 us
    reduce_scatter x1, waiting for transfers between devices, body(): lax.psum_scatter(jnp.dot(attended, w_out, preferred_element_type=jnp.floa...  87.7 us
    unnamed x21, local copies, waits for them, and re-layouts  27.4 us
    dot_general x1, matrix products, body(): jnp.dot(block_rows, weights_flat, preferred_element_type=jnp.float32)  25.8 us
    dot_general x5, matrix products, one_block(): jnp.einsum('hqk,khe->qhe', weights, seq_value, preferred_element_type=jnp...  21.6 us
    sub x5, matrix products, one_block(): raised = jnp.exp(scores - row_max)  14.3 us
    dot_general x1, matrix products, body(): jnp.dot(attended, w_out, preferred_element_type=jnp.float32)  14.1 us
    transpose x2, local copies, waits for them, and re-layouts, write_cache(): jnp.moveaxis(key_value, 1, 0)  6.97 us
  transfers between devices with their start and end apart: 2, of which 2 were waited for; matrix products, arithmetic and copies ran while one was open for 11% of the time, Pallas kernels for 0%

commit v1 on v0

--- a/solution.py
+++ b/solution.py
@@ -74,7 +74,9 @@
     weights_flat = w_qkv.reshape(model_width, 3 * local_feat)
     bias_flat = b_qkv.reshape(-1)
     normed = layer_norm(tokens, ln_gain, ln_bias)
-    block_rows = lax.all_gather(normed, "tp", axis=0, tiled=True)
+    block_rows = jnp.concatenate(
+        lax.all_to_all(jnp.stack([normed] * lax.axis_size("tp")), "tp", 0, 0), axis=0
+    )
     result = jnp.dot(block_rows, weights_flat, preferred_element_type=jnp.float32) + bias_flat
     projected = result.astype(jnp.bfloat16).reshape(block_rows.shape[0], 3, local_feat)
     all_rows = projected.shape[0]

time: 336 us -> 474 us (1.41)
  waiting for transfers between devices: 177 us -> 302 us
  starting transfers between devices: 0.08 us -> 8.07 us
  local copies, waits for them, and re-layouts: 51 us -> 56.9 us
    all_to_all x0 -> x1, waiting for transfers between devices: none -> 215 us  [body(): lax.all_to_all(jnp.stack([normed] * lax.axis_size('tp')), 'tp', 0, 0)]
    all_gather x1 -> x0, waiting for transfers between devices: 89.7 us -> none  [body(): block_rows = lax.all_gather(normed, 'tp', axis=0, tiled=True)]
    all_to_all x0 -> x1, starting transfers between devices: none -> 8.03 us  [body(): lax.all_to_all(jnp.stack([normed] * lax.axis_size('tp')), 'tp', 0, 0)]
    another operation x0 -> x1, local copies, waits for them, and re-layouts: none -> 5.66 us  [body(): jnp.stack([normed] * lax.axis_size('tp'))]
  transfers between devices with their start and end apart: 2 -> 2, of which waited for: 2 -> 2; matrix products, arithmetic and copies ran while one was open for 11% -> 8% of each run, Pallas kernels for 0% -> 0%
where the time goes in v1:
time: 474 us; the launch traced here: 472 us
  waiting for transfers between devices  302 us (64%)
  matrix products  75.7 us (16%)
  local copies, waits for them, and re-layouts  56.9 us (12%)
  between operations  14.8 us (3%)
  other arithmetic  11.9 us (3%)
  starting transfers between devices  8.07 us (2%)
    all_to_all x1, waiting for transfers between devices, body(): lax.all_to_all(jnp.stack([normed] * lax.axis_size('tp')), 'tp', 0, 0)  215 us
    reduce_scatter x1, waiting for transfers between devices, body(): lax.psum_scatter(jnp.dot(attended, w_out, preferred_element_type=jnp.floa...  86.1 us
    unnamed x21, local copies, waits for them, and re-layouts  27.3 us
    dot_general x1, matrix products, body(): jnp.dot(block_rows, weights_flat, preferred_element_type=jnp.float32)  25.8 us
    dot_general x5, matrix products, one_block(): jnp.einsum('hqk,khe->qhe', weights, seq_value, preferred_element_type=jnp...  21.6 us
    sub x5, matrix products, one_block(): raised = jnp.exp(scores - row_max)  14.3 us
    dot_general x1, matrix products, body(): jnp.dot(attended, w_out, preferred_element_type=jnp.float32)  14.1 us
  transfers between devices with their start and end apart: 2, of which 2 were waited for; matrix products, arithmetic and copies ran while one was open for 8% of the time, Pallas kernels for 0%

profile of v1, /device:TPU:0, one launch (start us, length us, event | category | flops | bytes accessed | tf_op | source)
XLA Modules:
  0.0 472.4 jit_solution(556247978357589500)
XLA Ops:
  10.2 5.7 %stack.2 = bf16[16,80,6144]{2,1,0:T(8,128)(2,1)} broadcast(bf16[80,6144]{1,0:T(8,128)(2,1)S(1)} %fusion.43), dimensions={1,2} | broadcast | bytes 16711680 | tf_op jit(solution)/shard_map/stack | solution.py:78
  15.9 8.0 %all-to-all-start = ((bf16[16,80,6144]{2,1,0:T(8,128)(2,1)}), bf16[16,80,6144]{2,1,0:T(8,128)(2,1)}, u32[]{:S(2)}, u32[]{:S(2)}) async-start(bf16[16,80,6144]{2,1,0:T(8,128)(2,1)} %stack.2), calls=%async_computation | async-start | bytes 31457280 | tf_op jit(solution)/shard_map/all_to_all | solution.py:78
  24.0 18.7 %copy.20 = bf16[6144,3,384]{0,2,1:T(8,128)(2,1)} copy(bf16[6144,3,384]{2,0,1:T(8,128)(2,1)} %param.15) | data formatting | bytes 28311552 | tf_op args[3]
  42.7 215.5 %all-to-all-done = bf16[16,80,6144]{2,1,0:T(8,128)(2,1)} async-done(((bf16[16,80,6144]{2,1,0:T(8,128)(2,1)}), bf16[16,80,6144]{2,1,0:T(8,128)(2,1)}, u32[]{:S(2)}, u32[]{:S(2)}) %all-to-all-start) | async-done | bytes 15728672 | tf_op jit(solution)/shard_map/all_to_all | solution.py:78
  258.1 25.8 %fusion.37 = bf16[1280,1152]{0,1:T(8,128)(2,1)S(1)} fusion(bf16[1280,6144]{1,0:T(8,128)(2,1)} %bitcast.1, bf16[6144,1152]{0,1:T(8,128)(2,1)} %bitcast.68, f32[1152]{0:T(1024)S(1)} %add.87), kind=kOutput, calls=%fused_computation.32 | convolution fusion | flops 18122342400 | bytes 32838144 | tf_op jit(solution)/shard_map/dot_general | solution.py:80
  286.3 3.5 reshape.193
  289.7 2.6 copy.22
  295.8 46.9 %while.19 = (s32[]{:T(128)}, bf16[5,256,3,128]{3,1,2,0:T(8,128)(2,1)}, s32[5]{0:T(128)S(1)}, s32[]{:T(128)}, bf16[5,256,3,128]{3,1,2,0:T(8,128)(2,1)}, /*index=5...) while((s32[]{:T(128)}, ...), condition=%wide.region_5.6_spmd.clone.clone, body=%wide.region_2.5_spmd.clone.clone.sunk | while | flops 764580608 | bytes 4534397 | solution.py:47
  298.0 2.9 fusion.72
  300.9 4.3 fusion.73
  307.4 2.9 fusion.72
  310.2 4.3 fusion.73
  316.8 2.9 fusion.72
  319.6 4.3 fusion.73
  326.2 2.9 fusion.72
  329.0 4.3 fusion.73
  335.5 2.9 fusion.72
  338.4 4.3 fusion.73
  344.8 14.1 %convolution_convert_fusion = bf16[1280,6144]{1,0:T(8,128)(2,1)} fusion(bf16[384,6144]{1,0:T(8,128)(2,1)} %param.17, bf16[160,8,3,128]{3,2,1,0:T(4,128)(2,1)S(1)} %bitcast.74), kind=kOutput, calls=%fused_computation.30 | convolution fusion | flops 6047662080 | bytes 21430272 | tf_op jit(solution)/shard_map/dot_general | solution.py:90
  361.8 3.0 slice_bitcast_fusion
  364.8 4.0 copy.26
  368.9 3.7 fusion.44
  372.6 4.5 scatter_fusion
  377.1 86.1 %reduce-scatter.2.cloned.1.call-done = bf16[80,6144]{1,0:T(8,128)(2,1)} async-done(((bf16[1280,6144]{1,0:T(8,128)(2,1)}), bf16[80,6144]{1,0:T(8,128)(2,1)}) %reduce-scatter.2.cloned.1.call-update) | async-done | bytes 983056 | tf_op jit(solution)/shard_map/reduce_scatter | solution.py:89
  (57 shorter events, 23.3 us)
Async XLA Ops:
  7.2 1.9 copy-start.1
  7.2 2.6 copy-start.4
  7.2 2.6 copy-start.3
  15.9 242.3 %all-to-all-start = ((bf16[16,80,6144]{2,1,0:T(8,128)(2,1)}), bf16[16,80,6144]{2,1,0:T(8,128)(2,1)}, u32[]{:S(2)}, u32[]{:S(2)}) async-start(bf16[16,80,6144]{2,1,0:T(8,128)(2,1)} %stack.2), calls=%async_computation | async-start | bytes 31457280 | tf_op jit(solution)/shard_map/all_to_all | solution.py:78
  23.9 439.3 %reduce-scatter.2.cloned.1.call-start = ((), (), s32[]{:S(2)}) async-start(), calls=%async_computation.2 | async-start | bytes 16711680 | tf_op jit(solution)/shard_map/reduce_scatter | solution.py:89
  24.0 18.7 %copy-start.6 = (f32[3,384]{1,0:T(4,128)S(1)}, f32[3,384]{1,0:T(4,128)}, u32[]{:S(2)}) copy-start(f32[3,384]{1,0:T(4,128)} %param.16) | copy-start | bytes 13828
  283.9 2.3 copy-start.2
  358.8 0.7 copy-start.7
  372.6 90.6 %copy-start.5 = (f32[6144]{0:T(1024)S(1)}, f32[6144]{0:T(1024)}, u32[]{:S(2)}) copy-start(f32[6144]{0:T(1024)} %param.18) | copy-start | bytes 73732
  377.1 88.4 %copy-start = (bf16[2,12,128,384]{3,2,1,0:T(8,128)(2,1)}, bf16[2,12,128,384]{3,2,1,0:T(8,128)(2,1)S(1)}, u32[]{:S(2)}) copy-start(bf16[2,12,128,384]{3,2,1,0:T(8,128)(2,1)S(1)} %scatter_fusion) | copy-start | bytes 7077892
Sparse Core Ops, SparseCore 0:
  359.0 104.2 reduce-scatter.1
